TPU v7x, 128 devices: a whole 4x4x4 slice. The times are simulated.
128 devices in a mesh: sample: 2 (over x_hi), space: 64 (over x_lo, y, z, core).
Axes of the slice: x: 4 (x_hi: 2, x_lo: 2; x = x_hi * 2 + x_lo), y: 4, z: 4, core: 2. Of those that a mesh axis runs over, the one named last changes fastest.
Arguments:
- volumes: bfloat16 [2, 256, 16, 64, 128], P('sample', 'space'), may hold values from -6 to 6
- fine_kernel: bfloat16 [27, 128, 128], replicated, may hold values from -0.109375 to 0.109375
- coarse_kernel: bfloat16 [27, 128, 256], replicated, may hold values from -0.109375 to 0.109375
- cotangent: bfloat16 [2, 128, 8, 32, 256], P('sample', 'space'), may hold values from -6 to 6
Outputs:
- coarse_out: bfloat16 [2, 128, 8, 32, 256], P('sample', 'space')
- fine_grad: float32 [128, 3456], P('space')
- coarse_grad: float32 [256, 3456], P('space')
All inputs are finite; a program needn't handle non-finite values.
Results may differ from a plain program's by a relative error of at most 0.014.
Values may be sent and summed in bfloat16 or wider, within the bound.
A program may use at most 128 MiB of HBM per device.

v0:
```python
import functools

import jax
import jax.numpy as jnp
from jax import lax
from jax.experimental import pallas as pl
from jax.experimental.pallas import tpu as pltpu
from jax.sharding import PartitionSpec as P

F32 = jnp.float32
BF16 = jnp.bfloat16
MESH = pl.DeviceIdType.MESH
NT = (((1,), (1,)), ((), ()))

COARSE_UNITS = (("z", tuple(range(14))), ("y", tuple(range(14, 27))))
FINE_UNITS = (
    ("z", ((0, 0), (0, 1), (0, 2), (1, 0))),
    ("y", ((1, 1), (1, 2), (2, 0))),
    ("z", ((2, 1), (2, 2))),
)


def fine_taps(groups):
    return tuple(9 * a + 3 * b + c for a, c in groups for b in range(3))


def mm(x, w):
    return jnp.dot(x, w, preferred_element_type=F32)


def mm_nt(x, w):
    return lax.dot_general(x, w, NT, preferred_element_type=F32)


def sigmoid(v):
    return 1.0 / (1.0 + jnp.exp(-v))


def up16(n):
    return -(-n // 16) * 16


def place():
    s = lax.axis_index("sample")
    i = lax.axis_index("space")
    return s, i // 32, (i // 8) % 4, (i // 2) % 4, i % 2


def device(s, xl, y, z, core):
    return (s, ((xl * 4 + y) * 4 + z) * 2 + core)


def moved(ds, dxl, dy, dz, dcore):
    s, xl, y, z, core = place()
    return device(
        (s + ds) % 2, (xl + dxl) % 2, (y + dy) % 4, (z + dz) % 4, (core + dcore) % 2
    )


def b_moves():
    return [
        (do, dxl, ds) for do in range(4) for dxl in range(2) for ds in range(2)
    ]


def permutation(rows, first, width):
    s, xl, y, z, core = place()
    m = lax.broadcasted_iota(jnp.int32, (rows, width), 0)
    o = lax.broadcasted_iota(jnp.int32, (rows, width), 1)
    r = width // 64
    group = m // r
    mxl = (group % 2 + xl) % 2
    other = (group // 2) % 4
    lead = (group // 8) % 4
    mcore = ((group // 32) % 2 + core) % 2
    if first == "z":
        mz, my = (lead + z) % 4, (other + y) % 4
    else:
        mz, my = (other + z) % 4, (lead + y) % 4
    shard = ((mxl * 4 + my) * 4 + mz) * 2 + mcore
    return (shard * r + m % r == o).astype(F32).astype(BF16)


class Unit:
    def __init__(self, index, first, taps, rows, refs):
        self.index, self.first, self.taps, self.rows = index, first, taps, rows
        (self.own, self.send0, self.recv0, self.keep, self.senda, self.recva,
         self.sendb, self.recvb, self.sem0, self.sema, self.semb) = refs
        self.half = 32 * rows
        self.chunk = 8 * rows
        self.fold = up16(len(taps) * rows)

    def put(self, j, value):
        lanes = pl.ds(j * 128, 128)
        self.own[:, lanes] = value[: self.half]
        self.send0[:, lanes] = value[self.half :].astype(BF16)

    def core_copy(self):
        return pltpu.make_async_remote_copy(
            self.send0, self.recv0, self.sem0.at[0], self.sem0.at[1],
            device_id=moved(0, 0, 0, 0, 1), device_id_type=MESH,
        )

    def lead(self, d):
        return moved(0, 0, 0, d, 0) if self.first == "z" else moved(0, 0, d, 0, 0)

    def a_copy(self, d):
        return pltpu.make_async_remote_copy(
            self.senda.at[d - 1], self.recva.at[d - 1],
            self.sema.at[0, d - 1], self.sema.at[1, d - 1],
            device_id=self.lead(d), device_id_type=MESH,
        )

    def b_copy(self, move):
        do, dxl, ds = move
        slot = do * 4 + dxl * 2 + ds - 1
        to = moved(ds, dxl, do, 0, 0) if self.first == "z" else moved(ds, dxl, 0, do, 0)
        return pltpu.make_async_remote_copy(
            self.sendb.at[do * 2 + dxl], self.recvb.at[slot],
            self.semb.at[0, slot], self.semb.at[1, slot],
            device_id=to, device_id_type=MESH,
        )

    def step_core(self):
        self.core_copy().start()

    def step_a(self):
        self.core_copy().wait()
        total = self.own[...] + self.recv0[...].astype(F32)
        self.keep[...] = total[: self.chunk]
        for d in range(1, 4):
            self.senda[d - 1] = total[d * self.chunk : (d + 1) * self.chunk].astype(BF16)
        for d in (2, 1, 3):
            self.a_copy(d).start()

    def step_b(self):
        total = self.keep[...]
        for d in range(1, 4):
            self.a_copy(d).wait()
        for d in range(1, 4):
            total = total + self.recva[d - 1].astype(F32)
        r = self.rows
        for q in range(8):
            rows = total[q * r : (q + 1) * r]
            pieces = [rows[:, j * 128 : (j + 1) * 128] for j in range(len(self.taps))]
            missing = self.fold - r * len(self.taps)
            if missing:
                pieces.append(jnp.zeros((missing, 128), F32))
            self.sendb[q] = jnp.concatenate(pieces, axis=0).astype(BF16)
        moves = b_moves()[1:]
        for move in sorted(moves, key=lambda m: -(m[0] % 2 + 2 * (m[0] == 2) + m[1] + 2 * m[2])):
            self.b_copy(move).start()

    def step_c(self, out):
        for move in b_moves()[1:]:
            self.b_copy(move).wait()
        total = None
        for do in range(4):
            for dxl in range(2):
                slot = do * 4 + dxl * 2 - 1
                near = self.sendb[0] if slot < 0 else self.recvb[slot]
                pair = near.astype(F32) + self.recvb[slot + 1].astype(F32)
                total = pair if total is None else total + pair
        r = self.rows
        for j, tap in enumerate(self.taps):
            out[:, tap * 128 : (tap + 1) * 128] = total[j * r : (j + 1) * r]


def unit_scratch(taps, rows):
    width, half, chunk = len(taps) * 128, 32 * rows, 8 * rows
    fold = up16(len(taps) * rows)
    return [
        pltpu.VMEM((half, width), F32),
        pltpu.VMEM((half, width), BF16),
        pltpu.VMEM((half, width), BF16),
        pltpu.VMEM((chunk, width), F32),
        pltpu.VMEM((3, chunk, width), BF16),
        pltpu.VMEM((3, chunk, width), BF16),
        pltpu.VMEM((8, fold, 128), BF16),
        pltpu.VMEM((15, fold, 128), BF16),
        pltpu.SemaphoreType.DMA((2,)),
        pltpu.SemaphoreType.DMA((2, 3)),
        pltpu.SemaphoreType.DMA((2, 15)),
    ]


def shift_rows(block, step, period):
    size = block.shape[0]
    row = lax.broadcasted_iota(jnp.int32, block.shape, 0) % period
    if step > 0:
        return jnp.where(row == 0, 0.0, pltpu.roll(block, 1, 0))
    return jnp.where(row == period - 1, 0.0, pltpu.roll(block, size - 1, 0))


def kernel(
    vol, fk_hbm, ck_hbm, ct_hbm,
    out_hbm, fine_out, coarse_out,
    v, fk, ck, ct, slope, pool, spr, pc, cd, cacc, outb, dt,
    sem_in, sem_out, sem_v, sem_p, sem_c,
    *unit_refs,
):
    s, i = lax.axis_index("sample"), lax.axis_index("space")
    left = (s, (i + 63) % 64)
    right = (s, (i + 1) % 64)
    units = []
    at = 0
    for index, (first, taps) in enumerate(COARSE_UNITS):
        units.append(Unit(index, first, taps, 4, unit_refs[at : at + 11]))
        at += 11
    for index, (first, groups) in enumerate(FINE_UNITS):
        units.append(Unit(index, first, fine_taps(groups), 2, unit_refs[at : at + 11]))
        at += 11
    coarse_units, fine_units = units[: len(COARSE_UNITS)], units[len(COARSE_UNITS) :]

    barrier = pltpu.get_barrier_semaphore()
    moves = {(ds, dxl, do, 0, 0) for do, dxl, ds in b_moves()}
    moves |= {(ds, dxl, 0, do, 0) for do, dxl, ds in b_moves()}
    moves.discard((0, 0, 0, 0, 0))
    moves.add((0, 0, 0, 0, 1))
    peers = [moved(*move) for move in sorted(moves)] + [left, right]
    for peer in peers:
        pl.semaphore_signal(barrier, inc=1, device_id=peer, device_id_type=MESH)

    def interior(e):
        return pltpu.make_async_copy(
            vol.at[:, :, e],
            v.at[1, pl.ds(1, 4), pl.ds(1, 8), :, pl.ds(e * 128, 128)],
            sem_in.at[e],
        )

    load_fk = pltpu.make_async_copy(fk_hbm, fk, sem_in.at[2])
    load_ck = pltpu.make_async_copy(ck_hbm, ck, sem_in.at[3])
    load_ct = pltpu.make_async_copy(ct_hbm, ct, sem_in.at[4])
    interior(0).start()
    interior(1).start()
    load_fk.start()
    load_ck.start()
    load_ct.start()

    def halo(side, e):
        return pltpu.make_async_remote_copy(
            vol.at[3 if side == 0 else 0, :, e],
            v.at[1, 0 if side == 0 else 5, pl.ds(1, 8), :, pl.ds(e * 128, 128)],
            sem_v.at[0, side, e], sem_v.at[1, side, e],
            device_id=right if side == 0 else left, device_id_type=MESH,
        )

    for c in range(3):
        for p in range(6):
            v[c, p, 0] = jnp.zeros((64, 256), BF16)
            v[c, p, 9] = jnp.zeros((64, 256), BF16)
        for p in range(4):
            pc[c, p, 0] = jnp.zeros((32, 128), BF16)
            pc[c, p, 9] = jnp.zeros((32, 128), BF16)
    for p in range(4):
        cd[p, 0] = jnp.zeros((32, 256), BF16)
        cd[p, 9] = jnp.zeros((32, 256), BF16)

    pl.semaphore_wait(barrier, len(peers))
    for side in range(2):
        for e in range(2):
            halo(side, e).start()

    def shift_fine(p):
        block = v[1, p, 1:9].reshape(512, 256).astype(F32)
        v[0, p, 1:9] = shift_rows(block, 1, 64).astype(BF16).reshape(8, 64, 256)
        v[2, p, 1:9] = shift_rows(block, -1, 64).astype(BF16).reshape(8, 64, 256)

    interior(0).wait()
    interior(1).wait()
    for p in range(1, 5):
        shift_fine(p)
    load_fk.wait()

    zero = jnp.zeros((128, 128), BF16)

    def beside(a, b):
        return jnp.concatenate([a, b], axis=1)

    def over(a, b):
        return jnp.concatenate([a, b], axis=0)

    def fine_forward(p):
        acc = None
        for a in range(3):
            for c in range(3):
                k0, k1, k2 = (fk[9 * a + 3 * b + c] for b in range(3))
                here = v[c, p + a, 1:9].reshape(512, 256)
                around = beside(
                    v[c, p + a, 0:8, :, 128:256].reshape(512, 128),
                    v[c, p + a, 2:10, :, 0:128].reshape(512, 128),
                )
                term = mm(here, over(beside(k1, k0), beside(k2, k1)))
                term = term + mm(around, over(beside(k0, zero), beside(zero, k2)))
                acc = term if acc is None else acc + term
        sig = sigmoid(acc)
        act = acc * sig
        slope[p] = sig + act * (1.0 - sig)
        return act[:, :128] + act[:, 128:]

    def shift_pooled(p):
        block = pc[1, p, 1:9].reshape(256, 128).astype(F32)
        pc[0, p, 1:9] = shift_rows(block, 1, 32).astype(BF16).reshape(8, 32, 128)
        pc[2, p, 1:9] = shift_rows(block, -1, 32).astype(BF16).reshape(8, 32, 128)

    def pool_plane(q):
        even = pool[q, pl.ds(0, 256, stride=2), :]
        odd = pool[q, pl.ds(1, 256, stride=2), :]
        pc[1, q + 1, 1:9] = ((even + odd) * 0.125).astype(BF16).reshape(8, 32, 128)

    def neighbour(ref, sems, side):
        return pltpu.make_async_remote_copy(
            ref.at[2 if side == 0 else 1, pl.ds(1, 8)],
            ref.at[0 if side == 0 else 3, pl.ds(1, 8)],
            sems.at[0, side], sems.at[1, side],
            device_id=right if side == 0 else left, device_id_type=MESH,
        )

    pool[0] = fine_forward(1)
    pool[1] = fine_forward(2)
    for side in range(2):
        for e in range(2):
            halo(side, e).wait()

    @pl.when(i == 0)
    def _():
        v[1, 0, 1:9] = jnp.zeros((8, 64, 256), BF16)

    @pl.when(i == 63)
    def _():
        v[1, 5, 1:9] = jnp.zeros((8, 64, 256), BF16)

    shift_fine(0)
    shift_fine(5)
    pool[0] = pool[0] + fine_forward(0)
    pool_plane(0)
    neighbour(pc.at[1], sem_p, 1).start()
    pool[1] = pool[1] + fine_forward(3)
    pool_plane(1)
    neighbour(pc.at[1], sem_p, 0).start()
    shift_pooled(1)
    shift_pooled(2)
    load_ck.wait()
    load_ct.wait()

    def piece(q, a, b, c):
        return pc[c, q + a, b : b + 8].reshape(256, 128)

    def coarse_part(q, planes):
        taps = [(a, b, c) for a in planes for b in range(3) for c in range(3)]
        acc = None
        for at in range(0, len(taps), 2):
            some = taps[at : at + 2]
            x = jnp.concatenate([piece(q, *tap) for tap in some], axis=1)
            w = jnp.concatenate([ck[9 * a + 3 * b + c] for a, b, c in some], axis=0)
            term = mm(x, w)
            acc = term if acc is None else acc + term
        return acc

    cacc[0] = coarse_part(0, (1, 2))
    cacc[1] = coarse_part(1, (0, 1))
    for side in range(2):
        neighbour(pc.at[1], sem_p, side).wait()

    @pl.when(i == 0)
    def _():
        pc[1, 0, 1:9] = jnp.zeros((8, 32, 128), BF16)

    @pl.when(i == 63)
    def _():
        pc[1, 3, 1:9] = jnp.zeros((8, 32, 128), BF16)

    shift_pooled(0)
    shift_pooled(3)
    for q in range(2):
        pre = cacc[q] + coarse_part(q, (0,) if q == 0 else (2,))
        sig = sigmoid(pre)
        act = pre * sig
        outb[q] = act.astype(BF16).reshape(8, 32, 256)
        grad = ct[q].reshape(256, 256).astype(F32)
        cd[q + 1, 1:9] = (grad * (sig + act * (1.0 - sig))).astype(BF16).reshape(8, 32, 256)
        neighbour(cd, sem_c, 1 - q).start()
    store_out = pltpu.make_async_copy(outb, out_hbm, sem_out)
    store_out.start()

    delta = cd[1:3, 1:9].reshape(512, 256)
    for unit in coarse_units:
        lhs = mm_nt(permutation(256, unit.first, 256), delta).astype(BF16)
        for at in range(0, len(unit.taps), 2):
            some = unit.taps[at : at + 2]
            x = jnp.concatenate(
                [
                    pc[t % 3, t // 9 : t // 9 + 2, t // 3 % 3 : t // 3 % 3 + 8].reshape(512, 128)
                    for t in some
                ],
                axis=1,
            )
            term = mm(lhs, x)
            for k in range(len(some)):
                unit.put(at + k, term[:, k * 128 : (k + 1) * 128])
        unit.step_core()

    def back_part(q, planes):
        near, far = None, None
        for a in planes:
            for b in range(3):
                t = 9 * a + 3 * b
                x = cd[q + 2 - a, 2 - b : 10 - b].reshape(256, 256)
                one = mm_nt(x, ck[t : t + 2].reshape(256, 256))
                two = mm_nt(x, ck[t + 2])
                near = one if near is None else near + one
                far = two if far is None else far + two
        return near, far

    near0, far0 = back_part(0, (0, 1))
    near1, far1 = back_part(1, (1, 2))
    cacc[0], cacc[1] = near0, near1
    spr[0, 0:256], spr[1, 0:256] = far0, far1
    for side in range(2):
        neighbour(cd, sem_c, side).wait()

    @pl.when(i == 0)
    def _():
        cd[0, 1:9] = jnp.zeros((8, 32, 256), BF16)

    @pl.when(i == 63)
    def _():
        cd[3, 1:9] = jnp.zeros((8, 32, 256), BF16)

    for unit in coarse_units:
        unit.step_a()

    for q in range(2):
        near, far = back_part(q, (2,) if q == 0 else (0,))
        near, far = near + cacc[q], far + spr[q, 0:256]
        grad = near[:, 128:] + shift_rows(near[:, :128], -1, 32) + shift_rows(far, 1, 32)
        grad = grad.astype(BF16).astype(F32) * 0.125
        spr[q, pl.ds(0, 256, stride=2), :] = grad
        spr[q, pl.ds(1, 256, stride=2), :] = grad

    orders = {}
    for k, first in enumerate(("z", "y")):
        one = permutation(128, first, 128)
        orders[first] = (k, over(beside(one, zero), beside(zero, one)))
    for p in range(4):
        wide = spr[p // 2]
        d = (beside(wide, wide) * slope[p]).astype(BF16)
        for k, pick in orders.values():
            dt[k, :, p * 512 : (p + 1) * 512] = mm_nt(pick, d).astype(BF16)

    def fine_unit(unit, groups):
        k = orders[unit.first][0]
        for j, (a, c) in enumerate(groups):
            lhs = dt[k]
            here = v[c, a : a + 4, 1:9].reshape(2048, 256)
            around = beside(
                v[c, a : a + 4, 0:8, :, 128:256].reshape(2048, 128),
                v[c, a : a + 4, 2:10, :, 0:128].reshape(2048, 128),
            )
            g1 = mm(lhs, here)
            g2 = mm(lhs, around)
            unit.put(3 * j, g1[128:, :128] + g2[:128, :128])
            unit.put(3 * j + 1, g1[:128, :128] + g1[128:, 128:])
            unit.put(3 * j + 2, g1[:128, 128:] + g2[128:, 128:])
        unit.step_core()

    fine_unit(fine_units[0], FINE_UNITS[0][1])
    for unit in coarse_units:
        unit.step_b()
    fine_unit(fine_units[1], FINE_UNITS[1][1])
    fine_units[0].step_a()
    fine_unit(fine_units[2], FINE_UNITS[2][1])
    fine_units[1].step_a()
    fine_units[0].step_b()
    fine_units[2].step_a()
    for unit in coarse_units:
        unit.step_c(coarse_out)
    fine_units[1].step_b()
    fine_units[2].step_b()
    for unit in fine_units:
        unit.step_c(fine_out)
    store_out.wait()


def shards(volumes, fine_kernel, coarse_kernel, cotangent):
    vol = volumes.reshape(4, 8, 2, 64, 128)
    any_spec = pl.BlockSpec(memory_space=pl.ANY)
    vmem = pl.BlockSpec(memory_space=pltpu.VMEM)
    scratch = [
        pltpu.VMEM((3, 6, 10, 64, 256), BF16),
        pltpu.VMEM((27, 128, 128), BF16),
        pltpu.VMEM((27, 128, 256), BF16),
        pltpu.VMEM((2, 8, 32, 256), BF16),
        pltpu.VMEM((4, 512, 256), F32),
        pltpu.VMEM((2, 512, 128), F32),
        pltpu.VMEM((2, 512, 128), F32),
        pltpu.VMEM((3, 4, 10, 32, 128), BF16),
        pltpu.VMEM((4, 10, 32, 256), BF16),
        pltpu.VMEM((2, 256, 256), F32),
        pltpu.VMEM((2, 8, 32, 256), BF16),
        pltpu.VMEM((2, 256, 2048), BF16),
        pltpu.SemaphoreType.DMA((5,)),
        pltpu.SemaphoreType.DMA,
        pltpu.SemaphoreType.DMA((2, 2, 2)),
        pltpu.SemaphoreType.DMA((2, 2)),
        pltpu.SemaphoreType.DMA((2, 2)),
    ]
    for _, taps in COARSE_UNITS:
        scratch += unit_scratch(taps, 4)
    for _, groups in FINE_UNITS:
        scratch += unit_scratch(fine_taps(groups), 2)
    out, fine, coarse = pl.pallas_call(
        kernel,
        out_shape=(
            jax.ShapeDtypeStruct((2, 8, 32, 256), BF16),
            jax.ShapeDtypeStruct((2, 3456), F32),
            jax.ShapeDtypeStruct((4, 3456), F32),
        ),
        in_specs=[any_spec] * 4,
        out_specs=(any_spec, vmem, vmem),
        scratch_shapes=scratch,
        compiler_params=pltpu.CompilerParams(
            collective_id=0, has_side_effects=True, vmem_limit_bytes=60 * 2**20
        ),
        name="unet_step",
    )(vol, fine_kernel, coarse_kernel, cotangent[0])
    return out[None], fine, coarse


def solution(mesh):
    in_specs = (
        P("sample", "space", None, None, None),
        P(),
        P(),
        P("sample", "space", None, None, None),
    )
    out_specs = (P("sample", "space", None, None, None), P("space", None), P("space", None))
    return jax.shard_map(
        shards, mesh=mesh, in_specs=in_specs, out_specs=out_specs, check_vma=False
    )
```

profile of v0, /device:TPU:0, one launch (start us, length us, event | category | flops | bytes accessed | tf_op | source)
XLA Modules:
  0.0 61.1 jit_solution(16692111411483049409)
XLA Ops:
  0.6 56.0 %unet_step.1 = (bf16[2,8,32,256]{3,2,1,0:T(8,128)(2,1)}, f32[2,3456]{1,0:T(2,128)}, f32[4,3456]{1,0:T(4,128)}) custom-call(bf16[4,8,2,64,128]{4,3,2,1,0:T(8,128)(2,1)} %bitcast.3, bf16[27,128,128]{2,1,0:T(8,128)(2,1)} %fk_hbm.1, bf16[27,128,256]{2,1,0:T(8,128)(2,1)} %ck_hbm.1, bf16[2,8,32,256]{3,2,1,0:T(8,128)(2,1)} %bitcast.5), custom_call_target="tpu_custom_call" | custom-call | tf_op jit(solution)/shard_map/unet_step/pallas_call | solution.py:512
  56.6 1.7 %copy.10 = bf16[1,2,8,32,256]{4,3,2,1,0:T(8,128)(2,1)} copy(bf16[1,2,8,32,256]{4,3,2,1,0:T(8,128)(2,1)} %bitcast.4) | data formatting | bytes 524288
  58.3 1.4 %copy.11 = f32[2,3456]{1,0:T(2,128)} copy(f32[2,3456]{1,0:T(2,128)} %get-tuple-element.13) | data formatting | bytes 55296
  59.6 1.4 %copy.12 = f32[4,3456]{1,0:T(4,128)} copy(f32[4,3456]{1,0:T(4,128)} %get-tuple-element.14) | data formatting | bytes 110592
where the time goes:
time: 61.3 us; the launch traced here: 61.1 us
  Pallas kernels  56 us (91%)
  local copies, waits for them, and re-layouts  4.46 us (7%)
  between operations  0.64 us (1%)
    pallas_call x1, Pallas kernels, shards(): pl.pallas_call(kernel, out_shape=(jax.ShapeDtypeStruct((2, 8, 32, 256), B...  56 us
    unnamed x3, local copies, waits for them, and re-layouts  4.46 us

commit v1 on v0

--- a/solution.py
+++ b/solution.py
@@ -1,5 +1,3 @@
-import functools
-
 import jax
 import jax.numpy as jnp
 from jax import lax
@@ -12,11 +10,14 @@
 MESH = pl.DeviceIdType.MESH
 NT = (((1,), (1,)), ((), ()))
 
-COARSE_UNITS = (("z", tuple(range(14))), ("y", tuple(range(14, 27))))
+COARSE_UNITS = (
+    ("z", True, False, tuple(range(14))),
+    ("y", True, False, tuple(range(14, 27))),
+)
 FINE_UNITS = (
-    ("z", ((0, 0), (0, 1), (0, 2), (1, 0))),
-    ("y", ((1, 1), (1, 2), (2, 0))),
-    ("z", ((2, 1), (2, 2))),
+    ("z", False, False, ((0, 0), (0, 1), (0, 2), (1, 0))),
+    ("y", False, False, ((1, 1), (1, 2), (2, 0))),
+    ("z", False, True, ((2, 1), (2, 2))),
 )
 
 
@@ -82,13 +83,16 @@
 
 
 class Unit:
-    def __init__(self, index, first, taps, rows, refs):
-        self.index, self.first, self.taps, self.rows = index, first, taps, rows
-        (self.own, self.send0, self.recv0, self.keep, self.senda, self.recva,
-         self.sendb, self.recvb, self.sem0, self.sema, self.semb) = refs
+    def __init__(self, first, ring, twice, taps, rows, refs):
+        self.first, self.ring, self.twice, self.taps, self.rows = first, ring, twice, taps, rows
+        (self.own, self.send0, self.recv0, self.senda, self.recva, self.sendb, self.recvb,
+         self.sendc, self.sem0, self.sema, self.semb, self.semc) = refs
         self.half = 32 * rows
         self.chunk = 8 * rows
         self.fold = up16(len(taps) * rows)
+        width = len(taps) * 128
+        low = len(taps) // 2 * 128
+        self.low, self.high = pl.ds(0, low), pl.ds(low, width - low)
 
     def put(self, j, value):
         lanes = pl.ds(j * 128, 128)
@@ -111,9 +115,20 @@
             device_id=self.lead(d), device_id_type=MESH,
         )
 
+    def r_copy(self, k):
+        slot, lanes, d = (
+            (1, self.low, 1), (1, self.high, 3), (0, self.high, 1), (2, self.low, 3),
+            (0, self.low, 1), (2, self.high, 3),
+        )[k]
+        return pltpu.make_async_remote_copy(
+            self.senda.at[slot, :, lanes], self.recva.at[slot, :, lanes],
+            self.sema.at[0, k], self.sema.at[1, k],
+            device_id=self.lead(d), device_id_type=MESH,
+        )
+
     def b_copy(self, move):
         do, dxl, ds = move
-        slot = do * 4 + dxl * 2 + ds - 1
+        slot = (do * 4 + dxl * 2 + ds if self.twice else do * 2 + dxl) - 1
         to = moved(ds, dxl, do, 0, 0) if self.first == "z" else moved(ds, dxl, 0, do, 0)
         return pltpu.make_async_remote_copy(
             self.sendb.at[do * 2 + dxl], self.recvb.at[slot],
@@ -121,49 +136,92 @@
             device_id=to, device_id_type=MESH,
         )
 
+    def c_copy(self):
+        return pltpu.make_async_remote_copy(
+            self.sendc.at[0], self.sendc.at[1], self.semc.at[0], self.semc.at[1],
+            device_id=moved(1, 0, 0, 0, 0), device_id_type=MESH,
+        )
+
+    def b_moves(self):
+        return [m for m in b_moves()[1:] if self.twice or m[2] == 0]
+
+    def rows_of(self, d):
+        return pl.ds(d * self.chunk, self.chunk)
+
     def step_core(self):
         self.core_copy().start()
 
     def step_a(self):
         self.core_copy().wait()
         total = self.own[...] + self.recv0[...].astype(F32)
-        self.keep[...] = total[: self.chunk]
-        for d in range(1, 4):
-            self.senda[d - 1] = total[d * self.chunk : (d + 1) * self.chunk].astype(BF16)
-        for d in (2, 1, 3):
-            self.a_copy(d).start()
+        self.own[...] = total
+        if self.ring:
+            self.senda[1] = self.own[self.rows_of(2), :].astype(BF16)
+            self.senda[0, :, self.high] = self.own[self.rows_of(1), self.high].astype(BF16)
+            self.senda[2, :, self.low] = self.own[self.rows_of(3), self.low].astype(BF16)
+            for k in range(4):
+                self.r_copy(k).start()
+        else:
+            for d in (2, 1, 3):
+                self.senda[d - 1] = self.own[self.rows_of(d), :].astype(BF16)
+                self.a_copy(d).start()
+
+    def step_ring(self):
+        for k in range(4):
+            self.r_copy(k).wait()
+        one = self.own[self.rows_of(1), self.low] + self.recva[1, :, self.low].astype(F32)
+        self.senda[0, :, self.low] = one.astype(BF16)
+        three = self.own[self.rows_of(3), self.high] + self.recva[1, :, self.high].astype(F32)
+        self.senda[2, :, self.high] = three.astype(BF16)
+        for k in range(4, 6):
+            self.r_copy(k).start()
 
     def step_b(self):
-        total = self.keep[...]
-        for d in range(1, 4):
-            self.a_copy(d).wait()
-        for d in range(1, 4):
-            total = total + self.recva[d - 1].astype(F32)
+        total = self.own[self.rows_of(0), :]
+        if self.ring:
+            for k in range(4, 6):
+                self.r_copy(k).wait()
+            total = total + self.recva[0].astype(F32) + self.recva[2].astype(F32)
+        else:
+            for d in range(1, 4):
+                self.a_copy(d).wait()
+            for d in range(1, 4):
+                total = total + self.recva[d - 1].astype(F32)
         r = self.rows
-        for q in range(8):
+        for q in (4, 5, 2, 3, 6, 7, 1, 0):
             rows = total[q * r : (q + 1) * r]
             pieces = [rows[:, j * 128 : (j + 1) * 128] for j in range(len(self.taps))]
             missing = self.fold - r * len(self.taps)
             if missing:
                 pieces.append(jnp.zeros((missing, 128), F32))
             self.sendb[q] = jnp.concatenate(pieces, axis=0).astype(BF16)
-        moves = b_moves()[1:]
-        for move in sorted(moves, key=lambda m: -(m[0] % 2 + 2 * (m[0] == 2) + m[1] + 2 * m[2])):
-            self.b_copy(move).start()
-
-    def step_c(self, out):
-        for move in b_moves()[1:]:
-            self.b_copy(move).wait()
-        total = None
-        for do in range(4):
-            for dxl in range(2):
-                slot = do * 4 + dxl * 2 - 1
-                near = self.sendb[0] if slot < 0 else self.recvb[slot]
-                pair = near.astype(F32) + self.recvb[slot + 1].astype(F32)
-                total = pair if total is None else total + pair
+            for move in self.b_moves():
+                if move[0] * 2 + move[1] == q:
+                    self.b_copy(move).start()
+
+    def emit(self, total, out):
         r = self.rows
         for j, tap in enumerate(self.taps):
             out[:, tap * 128 : (tap + 1) * 128] = total[j * r : (j + 1) * r]
+
+    def step_c(self, out):
+        for move in self.b_moves():
+            self.b_copy(move).wait()
+        total = self.sendb[0].astype(F32)
+        if self.twice:
+            total = total + self.recvb[0].astype(F32)
+            for k in range(1, 14, 2):
+                total = total + (self.recvb[k].astype(F32) + self.recvb[k + 1].astype(F32))
+            self.emit(total, out)
+        else:
+            for k in range(7):
+                total = total + self.recvb[k].astype(F32)
+            self.sendc[0] = total.astype(BF16)
+            self.c_copy().start()
+
+    def step_d(self, out):
+        self.c_copy().wait()
+        self.emit(self.sendc[0].astype(F32) + self.sendc[1].astype(F32), out)
 
 
 def unit_scratch(taps, rows):
@@ -173,14 +231,15 @@
         pltpu.VMEM((half, width), F32),
         pltpu.VMEM((half, width), BF16),
         pltpu.VMEM((half, width), BF16),
-        pltpu.VMEM((chunk, width), F32),
         pltpu.VMEM((3, chunk, width), BF16),
         pltpu.VMEM((3, chunk, width), BF16),
         pltpu.VMEM((8, fold, 128), BF16),
         pltpu.VMEM((15, fold, 128), BF16),
+        pltpu.VMEM((2, fold, 128), BF16),
         pltpu.SemaphoreType.DMA((2,)),
-        pltpu.SemaphoreType.DMA((2, 3)),
+        pltpu.SemaphoreType.DMA((2, 6)),
         pltpu.SemaphoreType.DMA((2, 15)),
+        pltpu.SemaphoreType.DMA((2,)),
     ]
 
 
@@ -195,7 +254,7 @@
 def kernel(
     vol, fk_hbm, ck_hbm, ct_hbm,
     out_hbm, fine_out, coarse_out,
-    v, fk, ck, ct, slope, pool, spr, pc, cd, cacc, outb, dt,
+    v, fk, ck, ct, slope, pool, spr, pc, cd, cacc, outb, dt, facc, ckt, picks,
     sem_in, sem_out, sem_v, sem_p, sem_c,
     *unit_refs,
 ):
@@ -204,12 +263,12 @@
     right = (s, (i + 1) % 64)
     units = []
     at = 0
-    for index, (first, taps) in enumerate(COARSE_UNITS):
-        units.append(Unit(index, first, taps, 4, unit_refs[at : at + 11]))
-        at += 11
-    for index, (first, groups) in enumerate(FINE_UNITS):
-        units.append(Unit(index, first, fine_taps(groups), 2, unit_refs[at : at + 11]))
-        at += 11
+    for *how, taps in COARSE_UNITS:
+        units.append(Unit(*how, taps, 4, unit_refs[at : at + 12]))
+        at += 12
+    for *how, groups in FINE_UNITS:
+        units.append(Unit(*how, fine_taps(groups), 2, unit_refs[at : at + 12]))
+        at += 12
     coarse_units, fine_units = units[: len(COARSE_UNITS)], units[len(COARSE_UNITS) :]
 
     barrier = pltpu.get_barrier_semaphore()
@@ -239,7 +298,7 @@
 
     def halo(side, e):
         return pltpu.make_async_remote_copy(
-            vol.at[3 if side == 0 else 0, :, e],
+            v.at[1, 4 if side == 0 else 1, pl.ds(1, 8), :, pl.ds(e * 128, 128)],
             v.at[1, 0 if side == 0 else 5, pl.ds(1, 8), :, pl.ds(e * 128, 128)],
             sem_v.at[0, side, e], sem_v.at[1, side, e],
             device_id=right if side == 0 else left, device_id_type=MESH,
@@ -256,18 +315,25 @@
         cd[p, 0] = jnp.zeros((32, 256), BF16)
         cd[p, 9] = jnp.zeros((32, 256), BF16)
 
+    def shift_fine(p):
+        block = v[1, p, 1:9].reshape(512, 256).astype(F32)
+        v[0, p, 1:9] = shift_rows(block, 1, 64).astype(BF16).reshape(8, 64, 256)
+        v[2, p, 1:9] = shift_rows(block, -1, 64).astype(BF16).reshape(8, 64, 256)
+
+    for k, first in enumerate(("z", "y")):
+        picks[k] = permutation(256, first, 256)
+        pick = permutation(128, first, 128)
+        none = jnp.zeros((128, 128), BF16)
+        picks[2 + k, 0:128, 0:128] = pick
+        picks[2 + k, 0:128, 128:256] = none
+        picks[2 + k, 128:256, 0:128] = none
+        picks[2 + k, 128:256, 128:256] = pick
+    interior(0).wait()
+    interior(1).wait()
     pl.semaphore_wait(barrier, len(peers))
     for side in range(2):
         for e in range(2):
             halo(side, e).start()
-
-    def shift_fine(p):
-        block = v[1, p, 1:9].reshape(512, 256).astype(F32)
-        v[0, p, 1:9] = shift_rows(block, 1, 64).astype(BF16).reshape(8, 64, 256)
-        v[2, p, 1:9] = shift_rows(block, -1, 64).astype(BF16).reshape(8, 64, 256)
-
-    interior(0).wait()
-    interior(1).wait()
     for p in range(1, 5):
         shift_fine(p)
     load_fk.wait()
@@ -280,9 +346,9 @@
     def over(a, b):
         return jnp.concatenate([a, b], axis=0)
 
-    def fine_forward(p):
+    def fine_part(p, planes):
         acc = None
-        for a in range(3):
+        for a in planes:
             for c in range(3):
                 k0, k1, k2 = (fk[9 * a + 3 * b + c] for b in range(3))
                 here = v[c, p + a, 1:9].reshape(512, 256)
@@ -293,6 +359,9 @@
                 term = mm(here, over(beside(k1, k0), beside(k2, k1)))
                 term = term + mm(around, over(beside(k0, zero), beside(zero, k2)))
                 acc = term if acc is None else acc + term
+        return acc
+
+    def fine_forward(p, acc):
         sig = sigmoid(acc)
         act = acc * sig
         slope[p] = sig + act * (1.0 - sig)
@@ -316,8 +385,10 @@
             device_id=right if side == 0 else left, device_id_type=MESH,
         )
 
-    pool[0] = fine_forward(1)
-    pool[1] = fine_forward(2)
+    pool[0] = fine_forward(1, fine_part(1, (0, 1, 2)))
+    pool[1] = fine_forward(2, fine_part(2, (0, 1, 2)))
+    facc[0] = fine_part(0, (1, 2))
+    facc[1] = fine_part(3, (0, 1))
     for side in range(2):
         for e in range(2):
             halo(side, e).wait()
@@ -332,10 +403,10 @@
 
     shift_fine(0)
     shift_fine(5)
-    pool[0] = pool[0] + fine_forward(0)
+    pool[0] = pool[0] + fine_forward(0, facc[0] + fine_part(0, (0,)))
     pool_plane(0)
     neighbour(pc.at[1], sem_p, 1).start()
-    pool[1] = pool[1] + fine_forward(3)
+    pool[1] = pool[1] + fine_forward(3, facc[1] + fine_part(3, (2,)))
     pool_plane(1)
     neighbour(pc.at[1], sem_p, 0).start()
     shift_pooled(1)
@@ -359,6 +430,8 @@
 
     cacc[0] = coarse_part(0, (1, 2))
     cacc[1] = coarse_part(1, (0, 1))
+    for t in range(27):
+        ckt[t // 3, :, t % 3 * 128 : t % 3 * 128 + 128] = ck[t].T
     for side in range(2):
         neighbour(pc.at[1], sem_p, side).wait()
 
@@ -385,7 +458,7 @@
 
     delta = cd[1:3, 1:9].reshape(512, 256)
     for unit in coarse_units:
-        lhs = mm_nt(permutation(256, unit.first, 256), delta).astype(BF16)
+        lhs = mm_nt(picks[0 if unit.first == "z" else 1], delta).astype(BF16)
         for at in range(0, len(unit.taps), 2):
             some = unit.taps[at : at + 2]
             x = jnp.concatenate(
@@ -404,10 +477,9 @@
         near, far = None, None
         for a in planes:
             for b in range(3):
-                t = 9 * a + 3 * b
                 x = cd[q + 2 - a, 2 - b : 10 - b].reshape(256, 256)
-                one = mm_nt(x, ck[t : t + 2].reshape(256, 256))
-                two = mm_nt(x, ck[t + 2])
+                one = mm(x, ckt[3 * a + b, :, 0:256])
+                two = mm(x, ckt[3 * a + b, :, 256:384])
                 near = one if near is None else near + one
                 far = two if far is None else far + two
         return near, far
@@ -438,18 +510,14 @@
         spr[q, pl.ds(0, 256, stride=2), :] = grad
         spr[q, pl.ds(1, 256, stride=2), :] = grad
 
-    orders = {}
-    for k, first in enumerate(("z", "y")):
-        one = permutation(128, first, 128)
-        orders[first] = (k, over(beside(one, zero), beside(zero, one)))
     for p in range(4):
         wide = spr[p // 2]
         d = (beside(wide, wide) * slope[p]).astype(BF16)
-        for k, pick in orders.values():
-            dt[k, :, p * 512 : (p + 1) * 512] = mm_nt(pick, d).astype(BF16)
+        for k in range(2):
+            dt[k, :, p * 512 : (p + 1) * 512] = mm_nt(picks[2 + k], d).astype(BF16)
 
     def fine_unit(unit, groups):
-        k = orders[unit.first][0]
+        k = 0 if unit.first == "z" else 1
         for j, (a, c) in enumerate(groups):
             lhs = dt[k]
             here = v[c, a : a + 4, 1:9].reshape(2048, 256)
@@ -464,22 +532,42 @@
             unit.put(3 * j + 2, g1[:128, 128:] + g2[128:, 128:])
         unit.step_core()
 
-    fine_unit(fine_units[0], FINE_UNITS[0][1])
+    fine_unit(fine_units[0], FINE_UNITS[0][-1])
+    for unit in coarse_units:
+        unit.step_ring()
+    fine_unit(fine_units[1], FINE_UNITS[1][-1])
+    fine_units[0].step_a()
+    fine_unit(fine_units[2], FINE_UNITS[2][-1])
+    fine_units[1].step_a()
     for unit in coarse_units:
         unit.step_b()
-    fine_unit(fine_units[1], FINE_UNITS[1][1])
-    fine_units[0].step_a()
-    fine_unit(fine_units[2], FINE_UNITS[2][1])
-    fine_units[1].step_a()
+    fine_units[2].step_a()
     fine_units[0].step_b()
-    fine_units[2].step_a()
+    fine_units[1].step_b()
+    fine_units[2].step_b()
     for unit in coarse_units:
         unit.step_c(coarse_out)
-    fine_units[1].step_b()
-    fine_units[2].step_b()
-    for unit in fine_units:
-        unit.step_c(fine_out)
+    fine_units[0].step_c(fine_out)
+    fine_units[1].step_c(fine_out)
+    for unit in coarse_units:
+        unit.step_d(coarse_out)
+    fine_units[0].step_d(fine_out)
+    fine_units[1].step_d(fine_out)
+    fine_units[2].step_c(fine_out)
     store_out.wait()
+
+
+def finish(*refs):
+    ins, outs, bufs, sem = refs[:3], refs[3:6], refs[6:9], refs[9]
+    reads = [pltpu.make_async_copy(ins[k], bufs[k], sem.at[0, k]) for k in range(3)]
+    writes = [pltpu.make_async_copy(bufs[k], outs[k], sem.at[1, k]) for k in range(3)]
+    for read in reads:
+        read.start()
+    for read, write in zip(reads, writes):
+        read.wait()
+        write.start()
+    for write in writes:
+        write.wait()
 
 
 def shards(volumes, fine_kernel, coarse_kernel, cotangent):
@@ -499,23 +587,27 @@
         pltpu.VMEM((2, 256, 256), F32),
         pltpu.VMEM((2, 8, 32, 256), BF16),
         pltpu.VMEM((2, 256, 2048), BF16),
+        pltpu.VMEM((2, 512, 256), F32),
+        pltpu.VMEM((9, 256, 384), BF16),
+        pltpu.VMEM((4, 256, 256), BF16),
         pltpu.SemaphoreType.DMA((5,)),
         pltpu.SemaphoreType.DMA,
         pltpu.SemaphoreType.DMA((2, 2, 2)),
         pltpu.SemaphoreType.DMA((2, 2)),
         pltpu.SemaphoreType.DMA((2, 2)),
     ]
-    for _, taps in COARSE_UNITS:
+    for *_, taps in COARSE_UNITS:
         scratch += unit_scratch(taps, 4)
-    for _, groups in FINE_UNITS:
+    for *_, groups in FINE_UNITS:
         scratch += unit_scratch(fine_taps(groups), 2)
-    out, fine, coarse = pl.pallas_call(
+    results = (
+        jax.ShapeDtypeStruct((2, 8, 32, 256), BF16),
+        jax.ShapeDtypeStruct((2, 3456), F32),
+        jax.ShapeDtypeStruct((4, 3456), F32),
+    )
+    made = pl.pallas_call(
         kernel,
-        out_shape=(
-            jax.ShapeDtypeStruct((2, 8, 32, 256), BF16),
-            jax.ShapeDtypeStruct((2, 3456), F32),
-            jax.ShapeDtypeStruct((4, 3456), F32),
-        ),
+        out_shape=results,
         in_specs=[any_spec] * 4,
         out_specs=(any_spec, vmem, vmem),
         scratch_shapes=scratch,
@@ -524,6 +616,15 @@
         ),
         name="unet_step",
     )(vol, fine_kernel, coarse_kernel, cotangent[0])
+    out, fine, coarse = pl.pallas_call(
+        finish,
+        out_shape=results,
+        in_specs=[any_spec] * 3,
+        out_specs=[any_spec] * 3,
+        scratch_shapes=[pltpu.VMEM(r.shape, r.dtype) for r in results]
+        + [pltpu.SemaphoreType.DMA((2, 3))],
+        name="finish",
+    )(*made)
     return out[None], fine, coarse
 
 

time: 61.3 us -> 54 us (0.88)
  local copies, waits for them, and re-layouts: 4.46 us -> 0 us
  Pallas kernels: 56 us -> 53.1 us
    unnamed x3 -> x0, local copies, waits for them, and re-layouts: 4.46 us -> none
    pallas_call x1 -> x2, Pallas kernels: 56 us -> 53.1 us  [the longest x1 51.3 us: shards(): pl.pallas_call(kernel, out_shape=results, in_specs=[any_spec] * 4, out_sp...]
where the time goes in v1:
time: 54 us; the launch traced here: 53.9 us
  Pallas kernels  53.1 us (98%)
  between operations  0.8 us (1%)
    pallas_call x1, Pallas kernels, shards(): pl.pallas_call(kernel, out_shape=results, in_specs=[any_spec] * 4, out_sp...  51.3 us
    pallas_call x1, Pallas kernels, shards(): pl.pallas_call(finish, out_shape=results, in_specs=[any_spec] * 3, out_sp...  1.72 us

profile of v1, /device:TPU:0, one launch (start us, length us, event | category | flops | bytes accessed | tf_op | source)
XLA Modules:
  0.0 53.9 jit_solution(16821644644568907611)
XLA Ops:
  0.6 51.3 %unet_step.1 = (bf16[2,8,32,256]{3,2,1,0:T(8,128)(2,1)}, f32[2,3456]{1,0:T(2,128)}, f32[4,3456]{1,0:T(4,128)}) custom-call(bf16[4,8,2,64,128]{4,3,2,1,0:T(8,128)(2,1)} %bitcast.3, bf16[27,128,128]{2,1,0:T(8,128)(2,1)} %fk_hbm.1, bf16[27,128,256]{2,1,0:T(8,128)(2,1)} %ck_hbm.1, bf16[2,8,32,256]{3,2,1,0:T(8,128)(2,1)} %bitcast.4), custom_call_target="tpu_custom_call" | custom-call | tf_op jit(solution)/shard_map/unet_step/pallas_call | solution.py:608
  52.0 1.7 %finish.1 = (bf16[2,8,32,256]{3,2,1,0:T(8,128)(2,1)}, f32[2,3456]{1,0:T(2,128)}, f32[4,3456]{1,0:T(4,128)}) custom-call(bf16[2,8,32,256]{3,2,1,0:T(8,128)(2,1)} %get-tuple-element.9.refs_0_, f32[2,3456]{1,0:T(2,128)} %get-tuple-element.10.refs_1_, f32[4,3456]{1,0:T(4,128)} %get-tuple-element.11.refs_2_), custom_call_target="tpu_custom_call" | custom-call | tf_op jit(solution)/shard_map/finish/pallas_call | solution.py:619

commit v2 on v1

--- a/solution.py
+++ b/solution.py
@@ -15,8 +15,8 @@
     ("y", True, False, tuple(range(14, 27))),
 )
 FINE_UNITS = (
-    ("z", False, False, ((0, 0), (0, 1), (0, 2), (1, 0))),
-    ("y", False, False, ((1, 1), (1, 2), (2, 0))),
+    ("z", False, True, ((0, 0), (0, 1), (0, 2), (1, 0))),
+    ("y", False, True, ((1, 1), (1, 2), (2, 0))),
     ("z", False, True, ((2, 1), (2, 2))),
 )
 
@@ -389,23 +389,25 @@
     pool[1] = fine_forward(2, fine_part(2, (0, 1, 2)))
     facc[0] = fine_part(0, (1, 2))
     facc[1] = fine_part(3, (0, 1))
-    for side in range(2):
-        for e in range(2):
-            halo(side, e).wait()
+    for e in range(2):
+        halo(0, e).wait_recv()
 
     @pl.when(i == 0)
     def _():
         v[1, 0, 1:9] = jnp.zeros((8, 64, 256), BF16)
 
+    shift_fine(0)
+    pool[0] = pool[0] + fine_forward(0, facc[0] + fine_part(0, (0,)))
+    pool_plane(0)
+    neighbour(pc.at[1], sem_p, 1).start()
+    for e in range(2):
+        halo(1, e).wait_recv()
+
     @pl.when(i == 63)
     def _():
         v[1, 5, 1:9] = jnp.zeros((8, 64, 256), BF16)
 
-    shift_fine(0)
     shift_fine(5)
-    pool[0] = pool[0] + fine_forward(0, facc[0] + fine_part(0, (0,)))
-    pool_plane(0)
-    neighbour(pc.at[1], sem_p, 1).start()
     pool[1] = pool[1] + fine_forward(3, facc[1] + fine_part(3, (2,)))
     pool_plane(1)
     neighbour(pc.at[1], sem_p, 0).start()
@@ -432,20 +434,14 @@
     cacc[1] = coarse_part(1, (0, 1))
     for t in range(27):
         ckt[t // 3, :, t % 3 * 128 : t % 3 * 128 + 128] = ck[t].T
-    for side in range(2):
-        neighbour(pc.at[1], sem_p, side).wait()
-
-    @pl.when(i == 0)
-    def _():
-        pc[1, 0, 1:9] = jnp.zeros((8, 32, 128), BF16)
-
-    @pl.when(i == 63)
-    def _():
-        pc[1, 3, 1:9] = jnp.zeros((8, 32, 128), BF16)
-
-    shift_pooled(0)
-    shift_pooled(3)
-    for q in range(2):
+    def coarse_plane(q):
+        neighbour(pc.at[1], sem_p, q).wait_recv()
+
+        @pl.when(i == 63 * q)
+        def _():
+            pc[1, 3 * q, 1:9] = jnp.zeros((8, 32, 128), BF16)
+
+        shift_pooled(3 * q)
         pre = cacc[q] + coarse_part(q, (0,) if q == 0 else (2,))
         sig = sigmoid(pre)
         act = pre * sig
@@ -453,6 +449,9 @@
         grad = ct[q].reshape(256, 256).astype(F32)
         cd[q + 1, 1:9] = (grad * (sig + act * (1.0 - sig))).astype(BF16).reshape(8, 32, 256)
         neighbour(cd, sem_c, 1 - q).start()
+
+    coarse_plane(0)
+    coarse_plane(1)
     store_out = pltpu.make_async_copy(outb, out_hbm, sem_out)
     store_out.start()
 
@@ -488,72 +487,86 @@
     near1, far1 = back_part(1, (1, 2))
     cacc[0], cacc[1] = near0, near1
     spr[0, 0:256], spr[1, 0:256] = far0, far1
-    for side in range(2):
-        neighbour(cd, sem_c, side).wait()
-
-    @pl.when(i == 0)
-    def _():
-        cd[0, 1:9] = jnp.zeros((8, 32, 256), BF16)
-
-    @pl.when(i == 63)
-    def _():
-        cd[3, 1:9] = jnp.zeros((8, 32, 256), BF16)
-
     for unit in coarse_units:
         unit.step_a()
 
-    for q in range(2):
+    def fine_planes(q):
+        neighbour(cd, sem_c, q).wait_recv()
+
+        @pl.when(i == 63 * q)
+        def _():
+            cd[3 * q, 1:9] = jnp.zeros((8, 32, 256), BF16)
+
         near, far = back_part(q, (2,) if q == 0 else (0,))
         near, far = near + cacc[q], far + spr[q, 0:256]
         grad = near[:, 128:] + shift_rows(near[:, :128], -1, 32) + shift_rows(far, 1, 32)
         grad = grad.astype(BF16).astype(F32) * 0.125
         spr[q, pl.ds(0, 256, stride=2), :] = grad
         spr[q, pl.ds(1, 256, stride=2), :] = grad
-
-    for p in range(4):
-        wide = spr[p // 2]
-        d = (beside(wide, wide) * slope[p]).astype(BF16)
-        for k in range(2):
-            dt[k, :, p * 512 : (p + 1) * 512] = mm_nt(picks[2 + k], d).astype(BF16)
-
-    def fine_unit(unit, groups):
-        k = 0 if unit.first == "z" else 1
-        for j, (a, c) in enumerate(groups):
-            lhs = dt[k]
-            here = v[c, a : a + 4, 1:9].reshape(2048, 256)
-            around = beside(
-                v[c, a : a + 4, 0:8, :, 128:256].reshape(2048, 128),
-                v[c, a : a + 4, 2:10, :, 0:128].reshape(2048, 128),
-            )
-            g1 = mm(lhs, here)
-            g2 = mm(lhs, around)
-            unit.put(3 * j, g1[128:, :128] + g2[:128, :128])
-            unit.put(3 * j + 1, g1[:128, :128] + g1[128:, 128:])
-            unit.put(3 * j + 2, g1[:128, 128:] + g2[128:, 128:])
-        unit.step_core()
-
-    fine_unit(fine_units[0], FINE_UNITS[0][-1])
+        wide = spr[q]
+        for p in (2 * q, 2 * q + 1):
+            d = (beside(wide, wide) * slope[p]).astype(BF16)
+            for k in range(2):
+                dt[k, :, p * 512 : (p + 1) * 512] = mm_nt(picks[2 + k], d).astype(BF16)
+
+    fine_planes(0)
+    fine_planes(1)
     for unit in coarse_units:
         unit.step_ring()
-    fine_unit(fine_units[1], FINE_UNITS[1][-1])
-    fine_units[0].step_a()
-    fine_unit(fine_units[2], FINE_UNITS[2][-1])
-    fine_units[1].step_a()
+
+    def before(a, c):
+        return v[c, a : a + 4, 0:8, :, 128:256].reshape(2048, 128)
+
+    def after(a, c):
+        return v[c, a : a + 4, 2:10, :, 0:128].reshape(2048, 128)
+
+    def fine_groups(unit, groups, at, count):
+        k = 0 if unit.first == "z" else 1
+        some = groups[at : at + count]
+        if count == 2:
+            low = mm(dt[k, 0:128], beside(*(before(*g) for g in some)))
+            high = mm(dt[k, 128:256], beside(*(after(*g) for g in some)))
+            lows = low[:, :128], low[:, 128:]
+            highs = high[:, :128], high[:, 128:]
+        else:
+            both = mm(dt[k], beside(before(*some[0]), after(*some[0])))
+            lows, highs = (both[:128, :128],), (both[128:, 128:],)
+        for j, (a, c) in enumerate(some):
+            mid = mm(dt[k], v[c, a : a + 4, 1:9].reshape(2048, 256))
+            tap = 3 * (at + j)
+            unit.put(tap, mid[128:, :128] + lows[j])
+            unit.put(tap + 1, mid[:128, :128] + mid[128:, 128:])
+            unit.put(tap + 2, mid[:128, 128:] + highs[j])
+    one, two, three = fine_units
+    groups = [unit[-1] for unit in FINE_UNITS]
+    fine_groups(one, groups[0], 0, 2)
+    fine_groups(one, groups[0], 2, 2)
+    one.step_core()
+    fine_groups(two, groups[1], 0, 2)
+    one.step_a()
+    fine_groups(two, groups[1], 2, 1)
+    two.step_core()
     for unit in coarse_units:
         unit.step_b()
-    fine_units[2].step_a()
-    fine_units[0].step_b()
-    fine_units[1].step_b()
-    fine_units[2].step_b()
+    fine_groups(three, groups[2], 0, 2)
+    three.step_core()
+    two.step_a()
+    three.step_a()
+    one.step_b()
+    two.step_b()
+    three.step_b()
     for unit in coarse_units:
         unit.step_c(coarse_out)
-    fine_units[0].step_c(fine_out)
-    fine_units[1].step_c(fine_out)
+    one.step_c(fine_out)
+    two.step_c(fine_out)
     for unit in coarse_units:
         unit.step_d(coarse_out)
-    fine_units[0].step_d(fine_out)
-    fine_units[1].step_d(fine_out)
-    fine_units[2].step_c(fine_out)
+    three.step_c(fine_out)
+    for side in range(2):
+        for e in range(2):
+            halo(side, e).wait_send()
+        neighbour(pc.at[1], sem_p, side).wait_send()
+        neighbour(cd, sem_c, side).wait_send()
     store_out.wait()
 
 

time: 54 us -> 51.8 us (0.959)
  Pallas kernels: 53.1 us -> 50.9 us
    pallas_call x1, Pallas kernels: 51.3 us -> 49.2 us  [shards(): pl.pallas_call(kernel, out_shape=results, in_specs=[any_spec] * 4, out_sp...]
where the time goes in v2:
time: 51.8 us; the launch traced here: 51.7 us
  Pallas kernels  50.9 us (98%)
  between operations  0.8 us (2%)
    pallas_call x1, Pallas kernels, shards(): pl.pallas_call(kernel, out_shape=results, in_specs=[any_spec] * 4, out_sp...  49.2 us
    pallas_call x1, Pallas kernels, shards(): pl.pallas_call(finish, out_shape=results, in_specs=[any_spec] * 3, out_sp...  1.72 us

profile of v2, /device:TPU:0, one launch (start us, length us, event | category | flops | bytes accessed | tf_op | source)
XLA Modules:
  0.0 51.7 jit_solution(16406452429676828331)
XLA Ops:
  0.6 49.2 %unet_step.1 = (bf16[2,8,32,256]{3,2,1,0:T(8,128)(2,1)}, f32[2,3456]{1,0:T(2,128)}, f32[4,3456]{1,0:T(4,128)}) custom-call(bf16[4,8,2,64,128]{4,3,2,1,0:T(8,128)(2,1)} %bitcast.3, bf16[27,128,128]{2,1,0:T(8,128)(2,1)} %fk_hbm.1, bf16[27,128,256]{2,1,0:T(8,128)(2,1)} %ck_hbm.1, bf16[2,8,32,256]{3,2,1,0:T(8,128)(2,1)} %bitcast.4), custom_call_target="tpu_custom_call" | custom-call | tf_op jit(solution)/shard_map/unet_step/pallas_call | solution.py:621
  49.8 1.7 %finish.1 = (bf16[2,8,32,256]{3,2,1,0:T(8,128)(2,1)}, f32[2,3456]{1,0:T(2,128)}, f32[4,3456]{1,0:T(4,128)}) custom-call(bf16[2,8,32,256]{3,2,1,0:T(8,128)(2,1)} %get-tuple-element.9.refs_0_, f32[2,3456]{1,0:T(2,128)} %get-tuple-element.10.refs_1_, f32[4,3456]{1,0:T(4,128)} %get-tuple-element.11.refs_2_), custom_call_target="tpu_custom_call" | custom-call | tf_op jit(solution)/shard_map/finish/pallas_call | solution.py:632

commit v3 on v2

--- a/solution.py
+++ b/solution.py
@@ -167,7 +167,7 @@
                 self.a_copy(d).start()
 
     def step_ring(self):
-        for k in range(4):
+        for k in range(2):
             self.r_copy(k).wait()
         one = self.own[self.rows_of(1), self.low] + self.recva[1, :, self.low].astype(F32)
         self.senda[0, :, self.low] = one.astype(BF16)
@@ -179,7 +179,7 @@
     def step_b(self):
         total = self.own[self.rows_of(0), :]
         if self.ring:
-            for k in range(4, 6):
+            for k in range(2, 6):
                 self.r_copy(k).wait()
             total = total + self.recva[0].astype(F32) + self.recva[2].astype(F32)
         else:
@@ -511,8 +511,6 @@
 
     fine_planes(0)
     fine_planes(1)
-    for unit in coarse_units:
-        unit.step_ring()
 
     def before(a, c):
         return v[c, a : a + 4, 0:8, :, 128:256].reshape(2048, 128)
@@ -542,16 +540,18 @@
     fine_groups(one, groups[0], 0, 2)
     fine_groups(one, groups[0], 2, 2)
     one.step_core()
+    for unit in coarse_units:
+        unit.step_ring()
     fine_groups(two, groups[1], 0, 2)
     one.step_a()
     fine_groups(two, groups[1], 2, 1)
     two.step_core()
-    for unit in coarse_units:
-        unit.step_b()
     fine_groups(three, groups[2], 0, 2)
     three.step_core()
     two.step_a()
     three.step_a()
+    for unit in coarse_units:
+        unit.step_b()
     one.step_b()
     two.step_b()
     three.step_b()

time: 51.8 us -> 49.9 us (0.963)
  Pallas kernels: 50.9 us -> 48.8 us
    pallas_call x1, Pallas kernels: 49.2 us -> 47.1 us  [shards(): pl.pallas_call(kernel, out_shape=results, in_specs=[any_spec] * 4, out_sp...]
where the time goes in v3:
time: 49.9 us; the launch traced here: 49.6 us
  Pallas kernels  48.8 us (98%)
  between operations  0.8 us (2%)
    pallas_call x1, Pallas kernels, shards(): pl.pallas_call(kernel, out_shape=results, in_specs=[any_spec] * 4, out_sp...  47.1 us
    pallas_call x1, Pallas kernels, shards(): pl.pallas_call(finish, out_shape=results, in_specs=[any_spec] * 3, out_sp...  1.72 us

profile of v3, /device:TPU:0, one launch (start us, length us, event | category | flops | bytes accessed | tf_op | source)
XLA Modules:
  0.0 49.6 jit_solution(13229511923694529373)
XLA Ops:
  0.6 47.1 %unet_step.1 = (bf16[2,8,32,256]{3,2,1,0:T(8,128)(2,1)}, f32[2,3456]{1,0:T(2,128)}, f32[4,3456]{1,0:T(4,128)}) custom-call(bf16[4,8,2,64,128]{4,3,2,1,0:T(8,128)(2,1)} %bitcast.3, bf16[27,128,128]{2,1,0:T(8,128)(2,1)} %fk_hbm.1, bf16[27,128,256]{2,1,0:T(8,128)(2,1)} %ck_hbm.1, bf16[2,8,32,256]{3,2,1,0:T(8,128)(2,1)} %bitcast.4), custom_call_target="tpu_custom_call" | custom-call | tf_op jit(solution)/shard_map/unet_step/pallas_call | solution.py:621
  47.7 1.7 %finish.1 = (bf16[2,8,32,256]{3,2,1,0:T(8,128)(2,1)}, f32[2,3456]{1,0:T(2,128)}, f32[4,3456]{1,0:T(4,128)}) custom-call(bf16[2,8,32,256]{3,2,1,0:T(8,128)(2,1)} %get-tuple-element.9.refs_0_, f32[2,3456]{1,0:T(2,128)} %get-tuple-element.10.refs_1_, f32[4,3456]{1,0:T(4,128)} %get-tuple-element.11.refs_2_), custom_call_target="tpu_custom_call" | custom-call | tf_op jit(solution)/shard_map/finish/pallas_call | solution.py:632

commit v4 on v3

--- a/solution.py
+++ b/solution.py
@@ -15,7 +15,7 @@
     ("y", True, False, tuple(range(14, 27))),
 )
 FINE_UNITS = (
-    ("z", False, True, ((0, 0), (0, 1), (0, 2), (1, 0))),
+    ("z", False, False, ((0, 0), (0, 1), (0, 2), (1, 0))),
     ("y", False, True, ((1, 1), (1, 2), (2, 0))),
     ("z", False, True, ((2, 1), (2, 2))),
 )
@@ -153,18 +153,25 @@
 
     def step_a(self):
         self.core_copy().wait()
-        total = self.own[...] + self.recv0[...].astype(F32)
-        self.own[...] = total
-        if self.ring:
-            self.senda[1] = self.own[self.rows_of(2), :].astype(BF16)
-            self.senda[0, :, self.high] = self.own[self.rows_of(1), self.high].astype(BF16)
-            self.senda[2, :, self.low] = self.own[self.rows_of(3), self.low].astype(BF16)
-            for k in range(4):
-                self.r_copy(k).start()
-        else:
+        if not self.ring:
             for d in (2, 1, 3):
-                self.senda[d - 1] = self.own[self.rows_of(d), :].astype(BF16)
+                self.senda[d - 1] = self.summed(d).astype(BF16)
                 self.a_copy(d).start()
+            self.own[self.rows_of(0), :] = self.summed(0)
+            return
+        self.senda[1] = self.summed(2).astype(BF16)
+        for k in range(2):
+            self.r_copy(k).start()
+        for d in (1, 3, 0):
+            self.own[self.rows_of(d), :] = self.summed(d)
+        self.senda[0, :, self.high] = self.own[self.rows_of(1), self.high].astype(BF16)
+        self.senda[2, :, self.low] = self.own[self.rows_of(3), self.low].astype(BF16)
+        for k in range(2, 4):
+            self.r_copy(k).start()
+
+    def summed(self, d):
+        rows = self.rows_of(d)
+        return self.own[rows, :] + self.recv0[rows, :].astype(F32)
 
     def step_ring(self):
         for k in range(2):
@@ -276,8 +283,8 @@
     moves |= {(ds, dxl, 0, do, 0) for do, dxl, ds in b_moves()}
     moves.discard((0, 0, 0, 0, 0))
     moves.add((0, 0, 0, 0, 1))
-    peers = [moved(*move) for move in sorted(moves)] + [left, right]
-    for peer in peers:
+    peers = [left, right] + [moved(*move) for move in sorted(moves)]
+    for peer in peers[:2]:
         pl.semaphore_signal(barrier, inc=1, device_id=peer, device_id_type=MESH)
 
     def interior(e):
@@ -295,6 +302,8 @@
     load_fk.start()
     load_ck.start()
     load_ct.start()
+    for peer in peers[2:]:
+        pl.semaphore_signal(barrier, inc=1, device_id=peer, device_id_type=MESH)
 
     def halo(side, e):
         return pltpu.make_async_remote_copy(
@@ -456,8 +465,11 @@
     store_out.start()
 
     delta = cd[1:3, 1:9].reshape(512, 256)
+    orders = {
+        first: mm_nt(picks[k], delta).astype(BF16) for k, first in enumerate(("z", "y"))
+    }
     for unit in coarse_units:
-        lhs = mm_nt(picks[0 if unit.first == "z" else 1], delta).astype(BF16)
+        lhs = orders[unit.first]
         for at in range(0, len(unit.taps), 2):
             some = unit.taps[at : at + 2]
             x = jnp.concatenate(
@@ -483,11 +495,11 @@
                 far = two if far is None else far + two
         return near, far
 
-    near0, far0 = back_part(0, (0, 1))
-    near1, far1 = back_part(1, (1, 2))
-    cacc[0], cacc[1] = near0, near1
-    spr[0, 0:256], spr[1, 0:256] = far0, far1
-    for unit in coarse_units:
+    cacc[0], spr[0, 0:256] = back_part(0, (0, 1))
+    for unit in coarse_units[: len(coarse_units) // 2]:
+        unit.step_a()
+    cacc[1], spr[1, 0:256] = back_part(1, (1, 2))
+    for unit in coarse_units[len(coarse_units) // 2 :]:
         unit.step_a()
 
     def fine_planes(q):
@@ -549,9 +561,9 @@
     fine_groups(three, groups[2], 0, 2)
     three.step_core()
     two.step_a()
-    three.step_a()
     for unit in coarse_units:
         unit.step_b()
+    three.step_a()
     one.step_b()
     two.step_b()
     three.step_b()
@@ -561,6 +573,7 @@
     two.step_c(fine_out)
     for unit in coarse_units:
         unit.step_d(coarse_out)
+    one.step_d(fine_out)
     three.step_c(fine_out)
     for side in range(2):
         for e in range(2):

time: 49.9 us -> 48.9 us (0.980)
  Pallas kernels: 48.8 us -> 48 us
    pallas_call x1, Pallas kernels: 47.1 us -> 46.3 us  [shards(): pl.pallas_call(kernel, out_shape=results, in_specs=[any_spec] * 4, out_sp...]
where the time goes in v4:
time: 48.9 us; the launch traced here: 48.8 us
  Pallas kernels  48 us (98%)
  between operations  0.8 us (2%)
    pallas_call x1, Pallas kernels, shards(): pl.pallas_call(kernel, out_shape=results, in_specs=[any_spec] * 4, out_sp...  46.3 us
    pallas_call x1, Pallas kernels, shards(): pl.pallas_call(finish, out_shape=results, in_specs=[any_spec] * 3, out_sp...  1.72 us

profile of v4, /device:TPU:0, one launch (start us, length us, event | category | flops | bytes accessed | tf_op | source)
XLA Modules:
  0.0 48.8 jit_solution(14422868979191660199)
XLA Ops:
  0.6 46.3 %unet_step.1 = (bf16[2,8,32,256]{3,2,1,0:T(8,128)(2,1)}, f32[2,3456]{1,0:T(2,128)}, f32[4,3456]{1,0:T(4,128)}) custom-call(bf16[4,8,2,64,128]{4,3,2,1,0:T(8,128)(2,1)} %bitcast.3, bf16[27,128,128]{2,1,0:T(8,128)(2,1)} %fk_hbm.1, bf16[27,128,256]{2,1,0:T(8,128)(2,1)} %ck_hbm.1, bf16[2,8,32,256]{3,2,1,0:T(8,128)(2,1)} %bitcast.4), custom_call_target="tpu_custom_call" | custom-call | tf_op jit(solution)/shard_map/unet_step/pallas_call | solution.py:634
  46.9 1.7 %finish.1 = (bf16[2,8,32,256]{3,2,1,0:T(8,128)(2,1)}, f32[2,3456]{1,0:T(2,128)}, f32[4,3456]{1,0:T(4,128)}) custom-call(bf16[2,8,32,256]{3,2,1,0:T(8,128)(2,1)} %get-tuple-element.9.refs_0_, f32[2,3456]{1,0:T(2,128)} %get-tuple-element.10.refs_1_, f32[4,3456]{1,0:T(4,128)} %get-tuple-element.11.refs_2_), custom_call_target="tpu_custom_call" | custom-call | tf_op jit(solution)/shard_map/finish/pallas_call | solution.py:645

commit v5 on v4

--- a/solution.py
+++ b/solution.py
@@ -550,10 +550,10 @@
     one, two, three = fine_units
     groups = [unit[-1] for unit in FINE_UNITS]
     fine_groups(one, groups[0], 0, 2)
+    coarse_units[0].step_ring()
     fine_groups(one, groups[0], 2, 2)
     one.step_core()
-    for unit in coarse_units:
-        unit.step_ring()
+    coarse_units[1].step_ring()
     fine_groups(two, groups[1], 0, 2)
     one.step_a()
     fine_groups(two, groups[1], 2, 1)

time: 48.9 us -> 49 us (level)
  no operation moved by 1% of the time
where the time goes in v5:
time: 49 us; the launch traced here: 48.9 us
  Pallas kernels  48.1 us (98%)
  between operations  0.8 us (2%)
    pallas_call x1, Pallas kernels, shards(): pl.pallas_call(kernel, out_shape=results, in_specs=[any_spec] * 4, out_sp...  46.4 us
    pallas_call x1, Pallas kernels, shards(): pl.pallas_call(finish, out_shape=results, in_specs=[any_spec] * 3, out_sp...  1.72 us

profile of v5, /device:TPU:0, one launch (start us, length us, event | category | flops | bytes accessed | tf_op | source)
XLA Modules:
  0.0 48.9 jit_solution(12233901421164753927)
XLA Ops:
  0.6 46.4 %unet_step.1 = (bf16[2,8,32,256]{3,2,1,0:T(8,128)(2,1)}, f32[2,3456]{1,0:T(2,128)}, f32[4,3456]{1,0:T(4,128)}) custom-call(bf16[4,8,2,64,128]{4,3,2,1,0:T(8,128)(2,1)} %bitcast.3, bf16[27,128,128]{2,1,0:T(8,128)(2,1)} %fk_hbm.1, bf16[27,128,256]{2,1,0:T(8,128)(2,1)} %ck_hbm.1, bf16[2,8,32,256]{3,2,1,0:T(8,128)(2,1)} %bitcast.4), custom_call_target="tpu_custom_call" | custom-call | tf_op jit(solution)/shard_map/unet_step/pallas_call | solution.py:634
  47.0 1.7 %finish.1 = (bf16[2,8,32,256]{3,2,1,0:T(8,128)(2,1)}, f32[2,3456]{1,0:T(2,128)}, f32[4,3456]{1,0:T(4,128)}) custom-call(bf16[2,8,32,256]{3,2,1,0:T(8,128)(2,1)} %get-tuple-element.9.refs_0_, f32[2,3456]{1,0:T(2,128)} %get-tuple-element.10.refs_1_, f32[4,3456]{1,0:T(4,128)} %get-tuple-element.11.refs_2_), custom_call_target="tpu_custom_call" | custom-call | tf_op jit(solution)/shard_map/finish/pallas_call | solution.py:645

commit v6 on v4

--- a/solution.py
+++ b/solution.py
@@ -574,13 +574,13 @@
     for unit in coarse_units:
         unit.step_d(coarse_out)
     one.step_d(fine_out)
-    three.step_c(fine_out)
     for side in range(2):
         for e in range(2):
             halo(side, e).wait_send()
         neighbour(pc.at[1], sem_p, side).wait_send()
         neighbour(cd, sem_c, side).wait_send()
     store_out.wait()
+    three.step_c(fine_out)
 
 
 def finish(*refs):

time: 48.9 us -> 48.9 us (level)
  no operation moved by 1% of the time
where the time goes in v6:
time: 48.9 us; the launch traced here: 48.8 us
  Pallas kernels  48 us (98%)
  between operations  0.8 us (2%)
    pallas_call x1, Pallas kernels, shards(): pl.pallas_call(kernel, out_shape=results, in_specs=[any_spec] * 4, out_sp...  46.3 us
    pallas_call x1, Pallas kernels, shards(): pl.pallas_call(finish, out_shape=results, in_specs=[any_spec] * 3, out_sp...  1.72 us

profile of v6, /device:TPU:0, one launch (start us, length us, event | category | flops | bytes accessed | tf_op | source)
XLA Modules:
  0.0 48.8 jit_solution(1297262922072180883)
XLA Ops:
  0.6 46.3 %unet_step.1 = (bf16[2,8,32,256]{3,2,1,0:T(8,128)(2,1)}, f32[2,3456]{1,0:T(2,128)}, f32[4,3456]{1,0:T(4,128)}) custom-call(bf16[4,8,2,64,128]{4,3,2,1,0:T(8,128)(2,1)} %bitcast.3, bf16[27,128,128]{2,1,0:T(8,128)(2,1)} %fk_hbm.1, bf16[27,128,256]{2,1,0:T(8,128)(2,1)} %ck_hbm.1, bf16[2,8,32,256]{3,2,1,0:T(8,128)(2,1)} %bitcast.4), custom_call_target="tpu_custom_call" | custom-call | tf_op jit(solution)/shard_map/unet_step/pallas_call | solution.py:634
  46.9 1.7 %finish.1 = (bf16[2,8,32,256]{3,2,1,0:T(8,128)(2,1)}, f32[2,3456]{1,0:T(2,128)}, f32[4,3456]{1,0:T(4,128)}) custom-call(bf16[2,8,32,256]{3,2,1,0:T(8,128)(2,1)} %get-tuple-element.9.refs_0_, f32[2,3456]{1,0:T(2,128)} %get-tuple-element.10.refs_1_, f32[4,3456]{1,0:T(4,128)} %get-tuple-element.11.refs_2_), custom_call_target="tpu_custom_call" | custom-call | tf_op jit(solution)/shard_map/finish/pallas_call | solution.py:645
